TPU v7x, 128 devices: a whole 4x4x4 slice. The times are simulated.
128 devices in a mesh: lat: 16 (over x, z), lon: 8 (over y, core).
Axes of the slice: x: 4, y: 4, z: 4, core: 2. Of those that a mesh axis runs over, the one named last changes fastest.
Arguments:
- increment: bfloat16 [32, 16, 144, 128], P('lat', 'lon'), may hold values from -6 to 6
- cotangent: bfloat16 [16, 8, 40, 144, 128], P('lat', 'lon'), may hold values from -6 to 6
- weights: bfloat16 [16, 8, 40, 16, 128, 128], P('lat', 'lon'), may hold values from -0.1875 to 0.1875
- source_ids: int32 [16, 8, 40, 16], P('lat', 'lon'), may hold values from 0 to 511, as said below
- counts: int32 [16, 8, 40], P('lat', 'lon'), may hold values from 0 to 16, as said below
Outputs:
- ocean: bfloat16 [16, 8, 40, 144, 128], P('lat', 'lon')
- atmos_adjoint: bfloat16 [32, 16, 144, 128], P('lat', 'lon')
Inputs may be any that keep to these rules, and one draw needn't show every extreme that they name: source_ids[i, j, t, k] = a * 16 + b with block row a between i * 2 - 1 and (i + 1) * 2, and block column b equal, modulo 16, to one of j * 2 - 1 to (j + 1) * 2. `counts`: every device's tile (i, j) has some target block with exactly 16 live slots.
All inputs are finite; a program needn't handle non-finite values.
Results may differ from a plain program's by a relative error of at most 0.001.
Values may be sent and summed in bfloat16 or wider, within the bound.
A program may use at most 192 MiB of HBM per device.

v0:
```python
import jax
import jax.numpy as jnp
from jax import lax
from jax.sharding import PartitionSpec as P


def from_behind(value, axis, by):
    peers = lax.axis_size(axis)
    return lax.ppermute(value, axis, [(i, (i + by) % peers) for i in range(peers)])


def passed_along(block, axis, distance):
    devices = range(lax.axis_size(axis))
    route = [(i - distance, i) for i in devices if i - distance in devices]
    return lax.ppermute(block, axis, route)


def with_halo(block, sides, width):
    for axis, dim in sides:
        count = lax.axis_size(axis)
        forward = [(i, i + 1) for i in range(count - 1)]
        forward.append((count - 1, 0))
        backward = [(target, source) for source, target in forward]
        low = lax.ppermute(
            lax.slice_in_dim(block, block.shape[dim] - width, None, axis=dim), axis, forward
        )
        high = lax.ppermute(lax.slice_in_dim(block, 0, width, axis=dim), axis, backward)
        block = jnp.concatenate([low, block, high], axis=dim)
    return block


def fold_lon(partial_value):
    from_west = from_behind(partial_value[:, -1:], "lon", 1)
    from_east = from_behind(partial_value[:, :1], "lon", -1)
    middle = partial_value[:, 1:-1]
    return middle.at[:, :1].add(from_west).at[:, -1:].add(from_east)


def fold_lat(partial_value):
    from_north = passed_along(partial_value[-1:], "lat", 1)
    from_south = passed_along(partial_value[:1], "lat", -1)
    middle = partial_value[1:-1]
    return middle.at[:1].add(from_north).at[-1:].add(from_south)


def body(increment, cotangent, weights, source_ids, counts):
    tile_side = increment.shape[0]
    level_rows = increment.shape[2]
    block_cells = increment.shape[3]
    lon_count = lax.axis_size("lon")
    cycle_blocks = tile_side * lon_count
    lat_index = lax.axis_index("lat")
    lon_index = lax.axis_index("lon")
    source_list = source_ids[0, 0]
    live_counts = counts[0, 0]
    blocks = weights[0, 0]
    cotan_local = cotangent[0, 0]
    slot_count = blocks.shape[1]
    block_row = source_list // cycle_blocks
    block_col = source_list % cycle_blocks
    ext_col = (block_col - lon_index * tile_side + 1 + cycle_blocks) % cycle_blocks
    ext_width = tile_side + 2
    ext_rows = tile_side + 2
    ext_row = block_row - lat_index * tile_side + 1
    ext_total = ext_rows * ext_width
    positions = ext_row * ext_width + ext_col
    slot_index = jnp.arange(slot_count, dtype=jnp.int32)[None, :]
    active = slot_index < live_counts[:, None]
    place_index = jnp.arange(ext_total, dtype=jnp.int32)[None, None, :]
    selector = jnp.logical_and(positions[:, :, None] == place_index, active[:, :, None])
    extended = with_halo(increment, (("lat", 0), ("lon", 1)), 1)
    flattened = extended.reshape(ext_total, level_rows, block_cells)
    picked = jnp.einsum(
        "tke,ews->tkws",
        selector.astype(jnp.bfloat16),
        flattened,
        preferred_element_type=jnp.float32,
    ).astype(jnp.bfloat16)
    ocean_sum = jnp.einsum("tkws,tksb->twb", picked, blocks, preferred_element_type=jnp.float32)
    contribution = jnp.einsum(
        "twb,tksb->tkws", cotan_local, blocks, preferred_element_type=jnp.float32
    )
    partial_value = jnp.einsum(
        "tke,tkws->ews",
        selector.astype(jnp.float32),
        contribution,
        precision=lax.Precision.HIGHEST,
        preferred_element_type=jnp.float32,
    )
    partial_value = partial_value.reshape(ext_rows, ext_width, level_rows, block_cells)
    result_blocks = fold_lat(fold_lon(partial_value))
    return (ocean_sum.astype(jnp.bfloat16)[None, None], result_blocks.astype(jnp.bfloat16))


def solution(mesh):
    placed = (
        P("lat", "lon", None, None),
        P("lat", "lon", None, None, None),
        P("lat", "lon", None, None, None, None),
        P("lat", "lon", None, None),
        P("lat", "lon", None),
    )
    return jax.shard_map(
        body,
        mesh=mesh,
        in_specs=placed,
        out_specs=(P("lat", "lon", None, None, None), P("lat", "lon", None, None)),
        check_vma=False,
    )
```

profile of v0, /device:TPU:6, one launch (start us, length us, event | category | flops | bytes accessed | tf_op | source)
XLA Modules:
  0.0 136.1 jit_solution(15042297549956392149)
XLA Ops:
  0.6 0.0 copy-start
  0.6 1.7 %fusion.41 = (bf16[1,2,144,128]{3,2,1,0:T(8,128)(2,1)}, bf16[1,2,144,128]{3,2,1,0:T(8,128)(2,1)}) fusion(bf16[2,2,144,128]{3,2,1,0:T(8,128)(2,1)} %param.13), kind=kLoop, calls=%fused_computation.57 | loop fusion | bytes 294912 | tf_op jit(solution)/shard_map/slice | solution.py:27
  2.3 1.9 %collective-permute-start = (bf16[1,2,144,128]{3,2,1,0:T(8,128)(2,1)}, bf16[1,2,144,128]{3,2,1,0:T(8,128)(2,1)}, u32[]{:S(2)}, u32[]{:S(2)}) collective-permute-start(bf16[1,2,144,128]{3,2,1,0:T(8,128)(2,1)} %get-tuple-element.58), channel_id=1, source_target_pairs={{0,8},{8,16},{16,24},{24,32},{32,40},{40,48},{48,56},{56,64},{64,7... | collective-permute-start | bytes 221192 | tf_op jit(solution)/shard_map/ppermute | solution.py:24
  4.3 2.4 %collective-permute-start.1 = (bf16[1,2,144,128]{3,2,1,0:T(8,128)(2,1)}, bf16[1,2,144,128]{3,2,1,0:T(8,128)(2,1)S(1)}, u32[]{:S(2)}, u32[]{:S(2)}) collective-permute-start(bf16[1,2,144,128]{3,2,1,0:T(8,128)(2,1)} %get-tuple-element.57), channel_id=1, source_target_pairs={{8,0},{16,8},{24,16},{32,24},{40,32},{48,40},{56,48},{64,56},{72,6... | collective-permute-start | bytes 221192 | tf_op jit(solution)/shard_map/ppermute | solution.py:27
  6.7 0.7 iota_compare_fusion.1
  7.3 23.1 %fusion.4 = f32[40,16,128,144]{2,3,1,0:T(8,128)} fusion(bf16[1,1,40,16,128,128]{5,4,3,2,1,0:T(8,128)(2,1)} %param.15, bf16[1,1,40,144,128]{4,3,2,1,0:T(8,128)(2,1)S(1)} %copy-done), kind=kOutput, calls=%fused_computation.5 | convolution fusion | flops 3019898880 | bytes 69632000 | tf_op jit(solution)/shard_map/twb,tksb->tkws/dot_general | solution.py:80
  30.5 0.0 copy-start.3
  30.5 0.0 slice-start
  30.5 0.0 slice-start.1
  30.5 58.3 %fusion = f32[16,144,128,1]{2,0,3,1:T(8,128)S(1)} fusion(f32[40,16,128,144]{2,3,1,0:T(8,128)} %fusion.4, s32[40,16]{0,1:T(8,128)S(1)} %fusion.31, pred[40,16]{0,1:T(8,128)(4,1)S(1)} %iota_compare_fusion.1), kind=kOutput, calls=%fused_computation | convolution fusion | flops 2264944640 | bytes 48368768 | tf_op jit(solution)/shard_map/tke,tkws->ews/dot_general | solution.py:83
  88.9 0.9 constant_dynamic-update-slice_fusion.2
  89.9 0.0 collective-permute-start.2
  89.9 2.9 %collective-permute-start.3 = (bf16[4,1,144,128]{3,2,1,0:T(8,128)(2,1)S(1)}, bf16[4,1,144,128]{3,2,1,0:T(8,128)(2,1)S(1)}, u32[]{:S(2)}, u32[]{:S(2)}) collective-permute-start(bf16[4,1,144,128]{3,2,1,0:T(8,128)(2,1)S(1)} %get-tuple-element.56), channel_id=1, source_target_pairs={{1,0},{2,1},{3,2},{4,3},{5,4},{6,5},{7,6},{0,7},{9,8},{10,9},{11,1... | collective-permute-start | bytes 442376 | tf_op jit(solution)/shard_map/ppermute | solution.py:27
  92.8 0.6 fusion.38
  93.4 0.0 slice-start.3
  93.5 0.0 collective-permute-start.4
  93.5 2.9 %collective-permute-start.5 = (f32[4,1,144,128]{3,2,1,0:T(8,128)S(1)}, f32[4,1,144,128]{3,2,1,0:T(8,128)S(1)}, u32[]{:S(2)}, u32[]{:S(2)}) collective-permute-start(f32[4,1,144,128]{3,2,1,0:T(8,128)S(1)} %copy.21), channel_id=1, source_target_pairs={{0,7},{1,0},{2,1},{3,2},{4,3},{5,4},{6,5},{7,6},{8,15},{9,8},{10,9... | collective-permute-start | bytes 884744 | tf_op jit(solution)/shard_map/ppermute | solution.py:9
  96.5 0.3 slice.164
  96.8 0.1 copy.18
  96.9 0.1 pad_maximum_fusion
  97.0 0.0 slice-start.4
  97.0 10.7 %fusion.13 = bf16[40,16,144,128]{3,0,2,1:T(8,128)(2,1)} fusion(bf16[16,144,128,1]{2,1,0,3:T(8,128)(2,1)S(1)} %bitcast.61, s32[40,16]{0,1:T(8,128)S(1)} %fusion.31, pred[40,16]{0,1:T(8,128)(4,1)S(1)} %iota_compare_fusion.1), kind=kOutput, calls=%fused_computation.12 | convolution fusion | flops 377507840 | bytes 24185984 | tf_op jit(solution)/shard_map/tke,ews->tkws/dot_general | solution.py:73
  107.8 0.1 fusion.15
  107.9 0.8 copy-done.2
  108.7 0.7 fusion.39
  109.4 2.0 %collective-permute-start.6 = (f32[1,2,144,128]{3,2,1,0:T(8,128)}, f32[1,2,144,128]{3,2,1,0:T(8,128)S(1)}, u32[]{:S(2)}, u32[]{:S(2)}) collective-permute-start(f32[1,2,144,128]{3,2,1,0:T(8,128)} %get-tuple-element.54), channel_id=1, source_target_pairs={{0,8},{8,16},{16,24},{24,32},{32,40},{40,48},{48,56},{56,64},{64,7... | collective-permute-start | bytes 442376 | tf_op jit(solution)/shard_map/ppermute | solution.py:15
  111.5 13.8 %fusion.10 = bf16[1,1,40,144,128]{4,3,2,1,0:T(8,128)(2,1)} fusion(bf16[1,1,40,16,128,128]{5,4,3,2,1,0:T(8,128)(2,1)S(1)} %bitcast.58, bf16[40,16,144,128]{3,0,2,1:T(8,128)(2,1)} %fusion.13), kind=kOutput, calls=%fused_computation.10 | convolution fusion | flops 3020636160 | bytes 46039040 | tf_op jit(solution)/shard_map/tkws,tksb->twb/dot_general | solution.py:79
  125.3 1.0 slice.169
  126.3 6.0 %collective-permute-start.7 = (f32[1,2,144,128]{3,2,1,0:T(8,128)}, f32[1,2,144,128]{3,2,1,0:T(8,128)S(1)}, u32[]{:S(2)}, u32[]{:S(2)}) collective-permute-start(f32[1,2,144,128]{3,2,1,0:T(8,128)} %get-tuple-element.53), channel_id=1, source_target_pairs={{8,0},{16,8},{24,16},{32,24},{40,32},{48,40},{56,48},{64,56},{72,6... | collective-permute-start | bytes 442376 | tf_op jit(solution)/shard_map/ppermute | solution.py:15
  132.4 0.9 fusion.18
  133.3 2.0 %collective-permute-done.7 = f32[1,2,144,128]{3,2,1,0:T(8,128)S(1)} collective-permute-done((f32[1,2,144,128]{3,2,1,0:T(8,128)}, f32[1,2,144,128]{3,2,1,0:T(8,128)S(1)}, u32[]{:S(2)}, u32[]{:S(2)}) %collective-permute-start.7) | collective-permute-done | bytes 147488 | tf_op jit(solution)/shard_map/ppermute | solution.py:15
  135.4 0.7 convert_element_type.13
  (29 shorter events, 0.2 us)
Async XLA Ops:
  0.6 6.7 %copy-start = (bf16[1,1,40,144,128]{4,3,2,1,0:T(8,128)(2,1)S(1)}, bf16[1,1,40,144,128]{4,3,2,1,0:T(8,128)(2,1)}, u32[]{:S(2)}) copy-start(bf16[1,1,40,144,128]{4,3,2,1,0:T(8,128)(2,1)} %param.14) | copy-start | bytes 4423684
  2.3 86.5 %collective-permute-start = (bf16[1,2,144,128]{3,2,1,0:T(8,128)(2,1)}, bf16[1,2,144,128]{3,2,1,0:T(8,128)(2,1)}, u32[]{:S(2)}, u32[]{:S(2)}) collective-permute-start(bf16[1,2,144,128]{3,2,1,0:T(8,128)(2,1)} %get-tuple-element.58), channel_id=1, source_target_pairs={{0,8},{8,16},{16,24},{24,32},{32,40},{40,48},{48,56},{56,64},{64,7... | collective-permute-start | bytes 221192 | tf_op jit(solution)/shard_map/ppermute | solution.py:24
  4.3 85.5 %collective-permute-start.1 = (bf16[1,2,144,128]{3,2,1,0:T(8,128)(2,1)}, bf16[1,2,144,128]{3,2,1,0:T(8,128)(2,1)S(1)}, u32[]{:S(2)}, u32[]{:S(2)}) collective-permute-start(bf16[1,2,144,128]{3,2,1,0:T(8,128)(2,1)} %get-tuple-element.57), channel_id=1, source_target_pairs={{8,0},{16,8},{24,16},{32,24},{40,32},{48,40},{56,48},{64,56},{72,6... | collective-permute-start | bytes 221192 | tf_op jit(solution)/shard_map/ppermute | solution.py:27
  7.3 23.1 %copy-start.4 = (s32[1,1,40,16]{2,3,1,0:T(8,128)S(1)}, s32[1,1,40,16]{2,3,1,0:T(8,128)}, u32[]{:S(2)}) copy-start(s32[1,1,40,16]{2,3,1,0:T(8,128)} %param.16) | copy-start | bytes 7684
  30.5 59.3 %copy-start.3 = (bf16[2,2,144,128]{3,2,1,0:T(8,128)(2,1)S(1)}, bf16[2,2,144,128]{3,2,1,0:T(8,128)(2,1)}, u32[]{:S(2)}) copy-start(bf16[2,2,144,128]{3,2,1,0:T(8,128)(2,1)} %param.13) | copy-start | bytes 442372
  30.5 81.0 %slice-start = ((s8[20971520]{0:T(1024)(128)(4,1)}), s8[4194304]{0:T(1024)(128)(4,1)S(1)}, s32[]{:S(2)}) async-start(s8[20971520]{0:T(1024)(128)(4,1)} %bitcast.57), calls=%async_computation | async-start | bytes 8388608
  30.5 81.0 %slice-start.1 = ((s8[20971520]{0:T(1024)(128)(4,1)}), s8[4194304]{0:T(1024)(128)(4,1)S(1)}, s32[]{:S(2)}) async-start(s8[20971520]{0:T(1024)(128)(4,1)} %bitcast.57), calls=%async_computation.1 | async-start | bytes 8388608
  30.5 81.0 %slice-start.2 = ((s8[20971520]{0:T(1024)(128)(4,1)}), s8[4194304]{0:T(1024)(128)(4,1)S(1)}, s32[]{:S(2)}) async-start(s8[20971520]{0:T(1024)(128)(4,1)} %bitcast.57), calls=%async_computation.2 | async-start | bytes 8388608
  89.9 7.1 %collective-permute-start.2 = (bf16[4,1,144,128]{3,2,1,0:T(8,128)(2,1)S(1)}, bf16[4,1,144,128]{3,2,1,0:T(8,128)(2,1)S(1)}, u32[]{:S(2)}, u32[]{:S(2)}) collective-permute-start(bf16[4,1,144,128]{3,2,1,0:T(8,128)(2,1)S(1)} %get-tuple-element.55), channel_id=1, source_target_pairs={{0,1},{1,2},{2,3},{3,4},{4,5},{5,6},{6,7},{7,0},{8,9},{9,10},{10,1... | collective-permute-start | bytes 442376 | tf_op jit(solution)/shard_map/ppermute | solution.py:24
  89.9 7.0 %collective-permute-start.3 = (bf16[4,1,144,128]{3,2,1,0:T(8,128)(2,1)S(1)}, bf16[4,1,144,128]{3,2,1,0:T(8,128)(2,1)S(1)}, u32[]{:S(2)}, u32[]{:S(2)}) collective-permute-start(bf16[4,1,144,128]{3,2,1,0:T(8,128)(2,1)S(1)} %get-tuple-element.56), channel_id=1, source_target_pairs={{1,0},{2,1},{3,2},{4,3},{5,4},{6,5},{7,6},{0,7},{9,8},{10,9},{11,1... | collective-permute-start | bytes 442376 | tf_op jit(solution)/shard_map/ppermute | solution.py:27
  93.4 18.1 %slice-start.3 = ((s8[20971520]{0:T(1024)(128)(4,1)}), s8[4194304]{0:T(1024)(128)(4,1)S(1)}, s32[]{:S(2)}) async-start(s8[20971520]{0:T(1024)(128)(4,1)} %bitcast.57), calls=%async_computation.3 | async-start | bytes 8388608
  93.5 14.3 %collective-permute-start.4 = (f32[4,1,144,128]{3,2,1,0:T(8,128)S(1)}, f32[4,1,144,128]{3,2,1,0:T(8,128)S(1)}, u32[]{:S(2)}, u32[]{:S(2)}) collective-permute-start(f32[4,1,144,128]{3,2,1,0:T(8,128)S(1)} %copy.20), channel_id=1, source_target_pairs={{0,1},{1,2},{2,3},{3,4},{4,5},{5,6},{6,7},{7,0},{8,9},{9,10},{10,1... | collective-permute-start | bytes 884744 | tf_op jit(solution)/shard_map/ppermute | solution.py:9
  93.5 14.3 %collective-permute-start.5 = (f32[4,1,144,128]{3,2,1,0:T(8,128)S(1)}, f32[4,1,144,128]{3,2,1,0:T(8,128)S(1)}, u32[]{:S(2)}, u32[]{:S(2)}) collective-permute-start(f32[4,1,144,128]{3,2,1,0:T(8,128)S(1)} %copy.21), channel_id=1, source_target_pairs={{0,7},{1,0},{2,1},{3,2},{4,3},{5,4},{6,5},{7,6},{8,15},{9,8},{10,9... | collective-permute-start | bytes 884744 | tf_op jit(solution)/shard_map/ppermute | solution.py:9
  97.0 14.5 %slice-start.4 = ((s8[20971520]{0:T(1024)(128)(4,1)}), s8[4194304]{0:T(1024)(128)(4,1)S(1)}, s32[]{:S(2)}) async-start(s8[20971520]{0:T(1024)(128)(4,1)} %bitcast.57), calls=%async_computation.4 | async-start | bytes 8388608
  107.9 0.8 copy-start.2
  109.4 26.6 %copy-start.1 = (bf16[1,1,40,144,128]{4,3,2,1,0:T(8,128)(2,1)S(1)}, bf16[1,1,40,144,128]{4,3,2,1,0:T(8,128)(2,1)}, u32[]{:S(2)}) copy-start(bf16[1,1,40,144,128]{4,3,2,1,0:T(8,128)(2,1)} %param.14) | copy-start | bytes 4423684
  109.4 22.9 %collective-permute-start.6 = (f32[1,2,144,128]{3,2,1,0:T(8,128)}, f32[1,2,144,128]{3,2,1,0:T(8,128)S(1)}, u32[]{:S(2)}, u32[]{:S(2)}) collective-permute-start(f32[1,2,144,128]{3,2,1,0:T(8,128)} %get-tuple-element.54), channel_id=1, source_target_pairs={{0,8},{8,16},{16,24},{24,32},{32,40},{40,48},{48,56},{56,64},{64,7... | collective-permute-start | bytes 442376 | tf_op jit(solution)/shard_map/ppermute | solution.py:15
  126.3 9.0 %collective-permute-start.7 = (f32[1,2,144,128]{3,2,1,0:T(8,128)}, f32[1,2,144,128]{3,2,1,0:T(8,128)S(1)}, u32[]{:S(2)}, u32[]{:S(2)}) collective-permute-start(f32[1,2,144,128]{3,2,1,0:T(8,128)} %get-tuple-element.53), channel_id=1, source_target_pairs={{8,0},{16,8},{24,16},{32,24},{40,32},{48,40},{56,48},{64,56},{72,6... | collective-permute-start | bytes 442376 | tf_op jit(solution)/shard_map/ppermute | solution.py:15
where the time goes:
time: 137 us; the launch traced here: 136 us
  matrix products  106 us (77%)
  starting transfers between devices  18.3 us (13%)
  local copies, waits for them, and re-layouts  6.28 us (5%)
  other arithmetic  2.5 us (2%)
  waiting for transfers between devices  2.04 us (1%)
    dot_general x1, matrix products, body(): jnp.einsum('tke,tkws->ews', selector.astype(jnp.float32), contribution, p...  58.3 us
    dot_general x1, matrix products, body(): jnp.einsum('twb,tksb->tkws', cotan_local, blocks, preferred_element_type=...  23.1 us
    dot_general x1, matrix products, body(): jnp.einsum('tkws,tksb->twb', picked, blocks, preferred_element_type=jnp.f...  13.8 us
    dot_general x1, matrix products, body(): jnp.einsum('tke,ews->tkws', selector.astype(jnp.bfloat16), flattened, pre...  10.7 us
    ppermute x2, starting transfers between devices, passed_along(): return lax.ppermute(block, axis, route)  8.07 us
    ppermute x2, starting transfers between devices, with_halo(): lax.ppermute(lax.slice_in_dim(block, 0, width, axis=dim), axis, backward)  5.33 us
    ppermute x2, starting transfers between devices, from_behind(): lax.ppermute(value, axis, [(i, (i + by) % peers) for i in range(peers)])  2.97 us
  transfers between devices with their start and end apart: 8, of which 1 were waited for; matrix products, arithmetic and copies ran while one was open for 81% of the time, Pallas kernels for 0%

commit v1 on v0

v1 whole, which is shorter than its diff:
```python
import functools

import jax
import jax.numpy as jnp
from jax import lax
from jax.experimental import pallas as pl
from jax.experimental.pallas import tpu as pltpu
from jax.sharding import PartitionSpec as P

MESH = pl.DeviceIdType.MESH
CHAINS = 4
GROUP = 4
RING = 4

HALO = [(r, c) for r in range(4) for c in range(4) if r in (0, 3) or c in (0, 3)]
STEP = {0: -1, 1: 0, 2: 0, 3: 1}
SEND_ORDER = sorted(range(len(HALO)), key=lambda h: STEP[HALO[h][0]] == 0)


def kernel(
    lat_count, lon_count, targets, slots,
    table, inc_hbm, cot_hbm, w_hbm, ocean_hbm, adj_hbm,
    wbuf, cot, ext, d0, d1, d2, d3, obuf, sendb, recvb, abuf,
    w_sem, cot_sem, own_sem, inc_send, inc_recv, adj_send, adj_recv, out_sem, adj_sem,
):
    lat = lax.axis_index("lat")
    lon = lax.axis_index("lon")
    chains = (d0, d1, d2, d3)
    groups = targets // GROUP
    quads = slots // CHAINS
    entries = targets * quads
    rows, cells = ext.shape[1], ext.shape[2]
    total = targets * slots

    def load_w(g, slot, tt):
        return pltpu.make_async_copy(
            w_hbm.at[0, 0, g * GROUP + tt], wbuf.at[slot, tt], w_sem.at[slot, tt]
        )

    def load_cot(g):
        return pltpu.make_async_copy(
            cot_hbm.at[0, 0, pl.ds(g * GROUP, GROUP)], cot.at[pl.ds(g * GROUP, GROUP)], cot_sem.at[g]
        )

    own = [
        pltpu.make_async_copy(inc_hbm.at[r], ext.at[pl.ds((r + 1) * 4 + 1, 2)], own_sem.at[r])
        for r in range(2)
    ]
    for copy in own:
        copy.start()
    for g in range(RING):
        load_cot(g).start()
        for tt in range(GROUP):
            load_w(g, g, tt).start()
    for g in range(RING, groups):
        load_cot(g).start()

    def exists(dlat):
        if dlat < 0:
            return lat > 0
        if dlat > 0:
            return lat < lat_count - 1
        return None

    def guarded(dlat, action):
        if dlat == 0:
            action()
        else:
            pl.when(exists(dlat))(action)

    def peer(dlat, dlon):
        return (lat + dlat, lax.rem(lon + dlon + lon_count, lon_count))

    barrier = pltpu.get_barrier_semaphore()
    around = [(a, b) for a in (-1, 0, 1) for b in (-1, 0, 1) if (a, b) != (0, 0)]
    for a, b in around:
        guarded(
            a,
            lambda a=a, b=b: pl.semaphore_signal(
                barrier, inc=1, device_id=peer(a, b), device_id_type=MESH
            ),
        )
    bands = exists(-1).astype(jnp.int32) + exists(1).astype(jnp.int32)
    pl.semaphore_wait(barrier, 2 + 3 * bands)

    zero = jnp.zeros((rows, cells), jnp.float32)
    ext[16] = zero.astype(ext.dtype)
    for d in chains:
        d[entries] = zero

    def inc_copy(h):
        r, c = HALO[h]
        dlat, dlon = -STEP[r], -STEP[c]
        src = (r - 1 + 2 * (-STEP[r])) + 1, (c - 1 + 2 * (-STEP[c])) + 1
        return dlat, pltpu.make_async_remote_copy(
            src_ref=ext.at[src[0] * 4 + src[1]],
            dst_ref=ext.at[r * 4 + c],
            send_sem=inc_send.at[h],
            recv_sem=inc_recv.at[h],
            device_id=peer(dlat, dlon),
            device_id_type=MESH,
        )

    def adj_copy(h):
        r, c = HALO[h]
        dlat, dlon = STEP[r], STEP[c]
        return dlat, pltpu.make_async_remote_copy(
            src_ref=sendb.at[h],
            dst_ref=recvb.at[h],
            send_sem=adj_send.at[h],
            recv_sem=adj_recv.at[h],
            device_id=peer(dlat, dlon),
            device_id_type=MESH,
        )

    for copy in own:
        copy.wait()
    for h in SEND_ORDER:
        dlat, copy = inc_copy(h)
        guarded(dlat, copy.start)

    def adjoint_group(g, carry):
        slot = lax.rem(g, RING)
        load_cot(g).wait()
        for tt in range(GROUP):
            load_w(g, slot, tt).wait()
        for tt in range(GROUP):
            t = g * GROUP + tt
            here = cot[t]
            for q in range(quads):
                w = wbuf[slot, tt, pl.ds(q * CHAINS, CHAINS)].reshape(CHAINS * cells, cells)
                product = lax.dot_general(
                    here, w, (((1,), (1,)), ((), ())), preferred_element_type=jnp.float32
                )
                for j in range(CHAINS):
                    before = table[total + t * slots + q * CHAINS + j]
                    chains[j][t * quads + q] = (
                        product[:, j * cells : (j + 1) * cells] + chains[j][before]
                    )

        @pl.when(g + RING < groups)
        def _():
            for tt in range(GROUP):
                load_w(g + RING, slot, tt).start()

        return carry

    lax.fori_loop(0, groups, adjoint_group, 0)

    def summed(position):
        parts = [chains[j][table[2 * total + position * CHAINS + j]] for j in range(CHAINS)]
        return (parts[0] + parts[1]) + (parts[2] + parts[3])

    for h in SEND_ORDER:
        r, c = HALO[h]
        sendb[h] = summed(r * 4 + c)
        dlat, copy = adj_copy(h)
        guarded(dlat, copy.start)

    for h in SEND_ORDER:
        dlat, copy = inc_copy(h)
        guarded(-dlat, copy.wait_recv)
        guarded(dlat, copy.wait_send)

    def ocean_copy(g):
        return pltpu.make_async_copy(
            obuf.at[pl.ds(g * GROUP, GROUP)], ocean_hbm.at[0, 0, pl.ds(g * GROUP, GROUP)], out_sem.at[g]
        )

    def forward_group(i, carry):
        g = groups - 1 - i
        slot = lax.rem(g, RING)

        @pl.when(g < groups - RING)
        def _():
            for tt in range(GROUP):
                load_w(g, slot, tt).wait()

        for tt in range(GROUP):
            t = g * GROUP + tt
            picked = jnp.concatenate([ext[table[t * slots + k]] for k in range(slots)], axis=1)
            w = wbuf[slot, tt].reshape(slots * cells, cells)
            obuf[t] = jnp.dot(picked, w, preferred_element_type=jnp.float32).astype(obuf.dtype)
        ocean_copy(g).start()

        @pl.when(g >= RING)
        def _():
            for tt in range(GROUP):
                load_w(g - RING, slot, tt).start()

        return carry

    lax.fori_loop(0, groups, forward_group, 0)

    index = {place: h for h, place in enumerate(HALO)}
    for dlat in (-1, 1):
        r = 0 if dlat < 0 else 3

        @pl.when(jnp.logical_not(exists(-dlat)))
        def _():
            for c in range(4):
                recvb[index[r, c]] = zero

    for h in SEND_ORDER:
        dlat, copy = adj_copy(h)
        guarded(-dlat, copy.wait_recv)
    for a in range(2):
        for b in range(2):
            far_r, far_c = (3 if a == 0 else 0), (3 if b == 0 else 0)
            value = summed((a + 1) * 4 + b + 1)
            value += recvb[index[far_r, b + 1]] + recvb[index[a + 1, far_c]]
            value += recvb[index[far_r, far_c]]
            abuf[a, b] = value.astype(abuf.dtype)
    final = pltpu.make_async_copy(abuf, adj_hbm, adj_sem)
    final.start()
    for h in SEND_ORDER:
        dlat, copy = adj_copy(h)
        guarded(dlat, copy.wait_send)
    for g in range(groups):
        ocean_copy(g).wait()
    final.wait()


def tables(source_ids, counts):
    ids = source_ids[0, 0]
    targets, slots = ids.shape
    quads = slots // CHAINS
    cycle = 2 * lax.axis_size("lon")
    row = ids // cycle - 2 * lax.axis_index("lat") + 1
    col = (ids % cycle - 2 * lax.axis_index("lon") + 1 + cycle) % cycle
    live = jnp.arange(slots, dtype=jnp.int32)[None, :] < counts[0, 0][:, None]
    position = jnp.where(live, row * 4 + col, 16)
    entries = targets * quads
    lanes = position.reshape(entries, CHAINS).T
    order = jnp.arange(entries, dtype=jnp.int32)
    same = (lanes[:, :, None] == lanes[:, None, :]) & (order[None, None, :] < order[None, :, None])
    before = jnp.max(jnp.where(same, order[None, None, :], -1), axis=2)
    before = jnp.where(before < 0, entries, before)
    places = jnp.arange(16, dtype=jnp.int32)
    final = jnp.max(
        jnp.where(lanes[:, None, :] == places[None, :, None], order[None, None, :], -1), axis=2
    )
    final = jnp.where(final < 0, entries, final)
    return jnp.concatenate(
        [position.reshape(-1), before.T.reshape(-1), final.T.reshape(-1)]
    )


def body(lat_count, lon_count, increment, cotangent, weights, source_ids, counts):
    targets, slots = weights.shape[2], weights.shape[3]
    rows, cells = increment.shape[2], increment.shape[3]
    table = tables(source_ids, counts)
    groups = targets // GROUP
    entries = targets * slots // CHAINS
    halo = len(HALO)
    any_space = pl.BlockSpec(memory_space=pl.ANY)
    dma = pltpu.SemaphoreType.DMA
    return pl.pallas_call(
        functools.partial(kernel, lat_count, lon_count, targets, slots),
        out_shape=(
            jax.ShapeDtypeStruct(cotangent.shape, jnp.bfloat16),
            jax.ShapeDtypeStruct(increment.shape, jnp.bfloat16),
        ),
        in_specs=[pl.BlockSpec(memory_space=pltpu.SMEM)] + [any_space] * 3,
        out_specs=(any_space, any_space),
        scratch_shapes=[
            pltpu.VMEM((RING, GROUP, slots, cells, cells), jnp.bfloat16),
            pltpu.VMEM((targets, rows, cells), jnp.bfloat16),
            pltpu.VMEM((17, rows, cells), jnp.bfloat16),
        ]
        + [pltpu.VMEM((entries + 1, rows, cells), jnp.float32)] * CHAINS
        + [
            pltpu.VMEM((targets, rows, cells), jnp.bfloat16),
            pltpu.VMEM((halo, rows, cells), jnp.float32),
            pltpu.VMEM((halo, rows, cells), jnp.float32),
            pltpu.VMEM((2, 2, rows, cells), jnp.bfloat16),
            dma((RING, GROUP)),
            dma((groups,)),
            dma((2,)),
            dma((halo,)),
            dma((halo,)),
            dma((halo,)),
            dma((halo,)),
            dma((groups,)),
            dma,
        ],
        compiler_params=pltpu.CompilerParams(
            collective_id=0, has_side_effects=True, vmem_limit_bytes=67043328
        ),
    )(table, increment, cotangent, weights)


def solution(mesh):
    placed = (
        P("lat", "lon", None, None),
        P("lat", "lon", None, None, None),
        P("lat", "lon", None, None, None, None),
        P("lat", "lon", None, None),
        P("lat", "lon", None),
    )
    return jax.shard_map(
        functools.partial(body, mesh.shape["lat"], mesh.shape["lon"]),
        mesh=mesh,
        in_specs=placed,
        out_specs=(P("lat", "lon", None, None, None), P("lat", "lon", None, None)),
        check_vma=False,
    )
```

time: 137 us -> 35.8 us (0.26)
  matrix products: 106 us -> 0 us
  Pallas kernels: 0 us -> 27.1 us
  starting transfers between devices: 18.3 us -> 0 us
  waiting for transfers between devices: 2.04 us -> 0 us
    dot_general x4 -> x0, matrix products: 106 us -> none  [the longest x1 58.3 us: body(): jnp.einsum('tke,tkws->ews', selector.astype(jnp.float32), contribution, p...]
    pallas_call x0 -> x1, Pallas kernels: none -> 27.1 us  [body(): pl.pallas_call(functools.partial(kernel, lat_count, lon_count, targets, s...]
    ppermute x8 -> x0, starting transfers between devices: 18.3 us -> none  [the longest x2 8.07 us: passed_along(): return lax.ppermute(block, axis, route)]
    slice x6 -> x0, local copies, waits for them, and re-layouts: 4.33 us -> none  [the longest x1 1.7 us: with_halo(): lax.slice_in_dim(block, 0, width, axis=dim)]
    unnamed x25 -> x5, local copies, waits for them, and re-layouts: 1.94 us -> 4.06 us
    ppermute x8 -> x0, waiting for transfers between devices: 2.04 us -> none  [the longest x2 2.03 us: passed_along(): return lax.ppermute(block, axis, route)]
  transfers between devices with their start and end apart: 8 -> 0, of which waited for: 1 -> 0; matrix products, arithmetic and copies ran while one was open for 81% -> 0% of each run, Pallas kernels for 0% -> 0%
where the time goes in v1:
time: 35.8 us; the launch traced here: 35.5 us
  Pallas kernels  27.1 us (76%)
  local copies, waits for them, and re-layouts  5.72 us (16%)
  other arithmetic  1.97 us (6%)
  between operations  0.73 us (2%)
    pallas_call x1, Pallas kernels, body(): pl.pallas_call(functools.partial(kernel, lat_count, lon_count, targets, s...  27.1 us
    unnamed x5, local copies, waits for them, and re-layouts  4.06 us
    lt x5, local copies, waits for them, and re-layouts, tables(): live = jnp.arange(slots, dtype=jnp.int32)[None, :] < counts[0, 0][:, None]  1.04 us
    lt x2, other arithmetic, tables(): live = jnp.arange(slots, dtype=jnp.int32)[None, :] < counts[0, 0][:, None]  0.74 us

profile of v1, /device:TPU:6, one launch (start us, length us, event | category | flops | bytes accessed | tf_op | source)
XLA Modules:
  0.0 35.5 jit_solution(9389410735137737235)
XLA Ops:
  0.6 0.7 %iota_compare_fusion.2 = pred[40,16]{1,0:T(8,128)(4,1)S(1)} fusion(s32[40]{0:T(128)} %bitcast.13), kind=kLoop, calls=%fused_computation.4 | loop fusion | flops 640 | bytes 800 | tf_op jit(solution)/shard_map/lt | solution.py:231
  1.4 0.1 lt.86
  1.5 0.8 %copy.23 = s32[1,1,40,16]{3,2,1,0:T(8,128)S(1)} copy(s32[1,1,40,16]{2,3,1,0:T(8,128)} %param.8) | data formatting | bytes 5120 | tf_op args[3]
  2.2 0.1 squeeze.5
  2.4 0.7 %lt.94 = s32[40,4]{1,0:T(8,128)S(1)} broadcast(s32[40]{0:T(128)} %bitcast.14), dimensions={0} | broadcast | bytes 800 | tf_op jit(solution)/shard_map/lt | solution.py:231
  3.1 0.1 lt.95
  3.2 0.1 squeeze.6
  3.3 0.1 copy.25
  3.4 0.1 lt.93
  3.5 0.4 %select_reduce_fusion = s32[4,160]{1,0:T(4,128)S(1)} fusion(s32[4,160]{1,0:T(4,128)S(1)} %fusion.16, pred[160,160]{1,0:T(8,128)(4,1)S(1)} %iota_compare_fusion), kind=kLoop, calls=%fused_computation | loop fusion | flops 408960 | bytes 30720 | tf_op jit(solution)/shard_map/reduce_max | solution.py:237
  3.9 0.2 select_reduce_fusion.1
  4.1 0.1 copy.30
  4.2 0.1 reshape.39
  4.3 0.1 copy.29
  4.4 0.1 reshape.38
  4.5 0.6 %pad_add_fusion.table = s32[1344]{0:T(1024)} fusion(s32[64]{0:T(128)S(1)} %reshape.39, s32[640]{0:T(1024)S(1)} %reshape.38, s32[640]{0:T(1024)S(1)} %fusion.4), kind=kLoop, calls=%fused_computation.6 | loop fusion | flops 2688 | bytes 10752 | tf_op jit(solution)/shard_map/concatenate | solution.py:244
  5.1 27.1 %shard_map.68 = (bf16[1,1,40,144,128]{4,3,2,1,0:T(8,128)(2,1)}, bf16[2,2,144,128]{3,2,1,0:T(8,128)(2,1)}) custom-call(s32[1344]{0:T(1024)} %pad_add_fusion.table, bf16[2,2,144,128]{3,2,1,0:T(8,128)(2,1)} %inc_hbm.1, bf16[1,1,40,144,128]{4,3,2,1,0:T(8,128)(2,1)} %cot_hbm.1, bf16[1,1,40,16,128,128]{5,4,3,2,1,0:T(8,128)(2,1)} %w_hbm.1), custom_call_target="tpu_custom_call" | custom-call | tf_op jit(solution)/shard_map/pallas_call | solution.py:258
  32.2 0.0 copy-start
  32.3 2.6 %copy.33 = bf16[1,1,40,144,128]{4,3,2,1,0:T(8,128)(2,1)} copy(bf16[1,1,40,144,128]{4,3,2,1,0:T(8,128)(2,1)} %get-tuple-element.4) | data formatting | bytes 2949120
  34.9 0.0 copy-done
  34.9 0.7 %copy.34 = bf16[2,2,144,128]{3,2,1,0:T(8,128)(2,1)} copy(bf16[2,2,144,128]{3,2,1,0:T(8,128)(2,1)S(1)} %copy-done) | data formatting | bytes 294912
  (7 shorter events, 0.1 us)
Async XLA Ops:
  32.2 2.6 %copy-start = (bf16[2,2,144,128]{3,2,1,0:T(8,128)(2,1)S(1)}, bf16[2,2,144,128]{3,2,1,0:T(8,128)(2,1)}, u32[]{:S(2)}) copy-start(bf16[2,2,144,128]{3,2,1,0:T(8,128)(2,1)} %get-tuple-element.5) | copy-start | bytes 442372

commit v2 on v1

v2 whole, which is shorter than its diff:
```python
import functools

import jax
import jax.numpy as jnp
from jax import lax
from jax.experimental import pallas as pl
from jax.experimental.pallas import tpu as pltpu
from jax.sharding import PartitionSpec as P

MESH = pl.DeviceIdType.MESH
CHAINS = 4
GROUP = 8
RING = 2
PIECES = 4
SYNC = 1

PARTS = [
    [(0, 1), (0, 2)], [(3, 1), (3, 2)], [(0, 0)], [(0, 3)], [(3, 0)], [(3, 3)],
    [(1, 0), (2, 0)], [(1, 3), (2, 3)],
]
HALO = [place for part in PARTS for place in part]
FIRST = [HALO.index(part[0]) for part in PARTS]
STEP = {0: -1, 1: 0, 2: 0, 3: 1}
LEVELS = 32767.0


def kernel(
    lat_count, lon_count, targets, slots,
    inc_hbm, cot_hbm, w_hbm, ids_hbm, counts_hbm, obuf, abuf,
    wbuf, cot, ext, d0, d1, d2, d3, sendq, recvq, sends, recvs, ids, live, square, drawn, table,
    w_sem, cot_sem, own_sem, inc_send, inc_recv, adj_send, adj_recv, ids_sem, table_sem,
):
    lat = lax.axis_index("lat")
    lon = lax.axis_index("lon")
    chains = (d0, d1, d2, d3)
    groups = targets // GROUP
    quads = slots // CHAINS
    entries = targets * quads
    rows, cells = ext.shape[1], ext.shape[2]

    def load_w(g, slot, tt):
        return pltpu.make_async_copy(
            w_hbm.at[0, 0, g * GROUP + tt], wbuf.at[slot, tt], w_sem.at[slot, tt]
        )

    def load_cot(g):
        return pltpu.make_async_copy(
            cot_hbm.at[0, 0, pl.ds(g * GROUP, GROUP)], cot.at[pl.ds(g * GROUP, GROUP)], cot_sem.at[g]
        )

    wanted = [
        pltpu.make_async_copy(ids_hbm.at[0, 0], ids, ids_sem.at[0]),
        pltpu.make_async_copy(counts_hbm.at[0], live, ids_sem.at[1]),
    ]
    for copy in wanted:
        copy.start()
    own = [
        pltpu.make_async_copy(inc_hbm.at[r], ext.at[pl.ds((r + 1) * 4 + 1, 2)], own_sem.at[r])
        for r in range(2)
    ]
    for copy in own:
        copy.start()
    load_cot(0).start()
    for tt in range(GROUP):
        load_w(0, 0, tt).start()

    def exists(dlat):
        if dlat < 0:
            return lat > 0
        if dlat > 0:
            return lat < lat_count - 1
        return None

    def guarded(dlat, action):
        if dlat == 0:
            action()
        else:
            pl.when(exists(dlat))(action)

    def peer(dlat, dlon):
        return (lat + dlat, lax.rem(lon + dlon + lon_count, lon_count))

    barrier = pltpu.get_barrier_semaphore()
    around = [(a, b) for a in (-1, 0, 1) for b in (-1, 0, 1) if (a, b) != (0, 0)]
    for a, b in around:
        guarded(
            a,
            lambda a=a, b=b: pl.semaphore_signal(
                barrier, inc=1, device_id=peer(a, b), device_id_type=MESH
            ),
        )
    zero = jnp.zeros((rows, cells), jnp.float32)
    ext[16] = zero.astype(ext.dtype)
    for d in chains:
        d[entries] = zero

    def inc_copy(h):
        r, c = HALO[h]
        dlat, dlon = -STEP[r], -STEP[c]
        src = (r - 1 + 2 * (-STEP[r])) + 1, (c - 1 + 2 * (-STEP[c])) + 1
        return dlat, pltpu.make_async_remote_copy(
            src_ref=ext.at[src[0] * 4 + src[1]],
            dst_ref=ext.at[r * 4 + c],
            send_sem=inc_send.at[h],
            recv_sem=inc_recv.at[h],
            device_id=peer(dlat, dlon),
            device_id_type=MESH,
        )

    def adj_copies(d):
        r, c = PARTS[d][0]
        dlat, dlon = STEP[r], (0 if len(PARTS[d]) > 1 and r in (0, 3) else STEP[c])
        here = pl.ds(FIRST[d], len(PARTS[d]))
        return dlat, [
            pltpu.make_async_remote_copy(
                src_ref=src.at[here],
                dst_ref=dst.at[here],
                send_sem=adj_send.at[kind, d],
                recv_sem=adj_recv.at[kind, d],
                device_id=peer(dlat, dlon),
                device_id_type=MESH,
            )
            for kind, (src, dst) in enumerate(((sends, recvs), (sendq, recvq)))
        ]

    def each(copies, action):
        def run():
            for copy in copies:
                getattr(copy, action)()

        return run

    def coded(h, value):
        folded = value.reshape(rows // 8, 8, cells)
        largest = jnp.maximum(jnp.max(jnp.abs(folded), axis=0), 1e-30)
        sends[h] = largest * (1.0 / LEVELS)
        levels = jnp.round(folded * (LEVELS / largest))
        sendq[h] = levels.reshape(rows, cells).astype(jnp.int32).astype(jnp.int16)

    def decoded(h):
        levels = recvq[h].astype(jnp.int32).astype(jnp.float32)
        return (levels.reshape(rows // 8, 8, cells) * recvs[h][None]).reshape(rows, cells)

    for copy in wanted:
        copy.wait()
    draw_tables(lat, lon, lon_count, targets, slots, ids, live, square, drawn)
    to_scalars = pltpu.make_async_copy(drawn, table, table_sem)
    to_scalars.start()
    for g in range(1, groups):
        load_cot(g).start()
        if g < RING:
            for tt in range(GROUP):
                load_w(g, g, tt).start()
    to_scalars.wait()

    def adjoint_group(g, carry):
        slot = lax.rem(g, RING)
        load_cot(g).wait()
        for tt in range(GROUP):
            load_w(g, slot, tt).wait()
        for tt in range(GROUP):
            t = g * GROUP + tt
            here = cot[t]
            for q in range(quads):
                w = wbuf[slot, tt, pl.ds(q * CHAINS, CHAINS)].reshape(CHAINS * cells, cells)
                product = lax.dot_general(
                    here, w, (((1,), (1,)), ((), ())), preferred_element_type=jnp.float32
                )
                for j in range(CHAINS):
                    before = table[slots + q * CHAINS + j, t]
                    chains[j][t * quads + q] = (
                        product[:, j * cells : (j + 1) * cells] + chains[j][before]
                    )

        @pl.when(g + RING < groups)
        def _():
            for tt in range(GROUP):
                load_w(g + RING, slot, tt).start()

        return carry

    lax.fori_loop(0, SYNC, adjoint_group, 0)
    bands = exists(-1).astype(jnp.int32) + exists(1).astype(jnp.int32)
    pl.semaphore_wait(barrier, 2 + 3 * bands)

    for copy in own:
        copy.wait()
    for h in range(len(HALO)):
        dlat, copy = inc_copy(h)
        guarded(dlat, copy.start)
    lax.fori_loop(SYNC, groups, adjoint_group, 0)

    def summed(position):
        parts = [chains[j][table[2 * slots + j, position]] for j in range(CHAINS)]
        return (parts[0] + parts[1]) + (parts[2] + parts[3])

    for d, part in enumerate(PARTS):
        for h, (r, c) in enumerate(part, FIRST[d]):
            coded(h, summed(r * 4 + c))
        dlat, copies = adj_copies(d)
        guarded(dlat, each(copies, "start"))

    for h in range(len(HALO)):
        dlat, copy = inc_copy(h)
        guarded(-dlat, copy.wait_recv)
        guarded(dlat, copy.wait_send)

    def forward_group(i, carry):
        g = groups - 1 - i
        slot = lax.rem(g, RING)

        @pl.when(g < groups - RING)
        def _():
            for tt in range(GROUP):
                load_w(g, slot, tt).wait()

        for tt in range(GROUP):
            t = g * GROUP + tt
            picked = jnp.concatenate([ext[table[k, t]] for k in range(slots)], axis=1)
            w = wbuf[slot, tt].reshape(slots * cells, cells)
            obuf[0, 0, t] = jnp.dot(picked, w, preferred_element_type=jnp.float32).astype(obuf.dtype)

        @pl.when(g >= RING)
        def _():
            for tt in range(GROUP):
                load_w(g - RING, slot, tt).start()

        return carry

    lax.fori_loop(0, groups, forward_group, 0)

    index = {place: h for h, place in enumerate(HALO)}
    for dlat in (-1, 1):
        r = 0 if dlat < 0 else 3

        @pl.when(jnp.logical_not(exists(-dlat)))
        def _():
            for c in range(4):
                recvq[index[r, c]] = jnp.zeros((rows, cells), recvq.dtype)
                recvs[index[r, c]] = jnp.zeros(recvs.shape[1:], recvs.dtype)

    for d in range(len(PARTS)):
        dlat, copies = adj_copies(d)
        guarded(-dlat, each(copies, "wait_recv"))
    for a in range(2):
        for b in range(2):
            far_r, far_c = (3 if a == 0 else 0), (3 if b == 0 else 0)
            value = summed((a + 1) * 4 + b + 1)
            value += decoded(index[far_r, b + 1]) + decoded(index[a + 1, far_c])
            value += decoded(index[far_r, far_c])
            abuf[a, b] = value.astype(abuf.dtype)
    for d in range(len(PARTS)):
        dlat, copies = adj_copies(d)
        guarded(dlat, each(copies, "wait_send"))


def draw_tables(lat, lon, lon_count, targets, slots, ids, live, square, drawn):
    quads = slots // CHAINS
    cycle = 2 * lon_count
    entries = targets * quads
    number = ids[...]
    row = number // cycle - 2 * lat + 1
    col = (number % cycle - 2 * lon + 1 + cycle) % cycle
    slot = lax.broadcasted_iota(jnp.int32, (slots, targets), 0)
    position = jnp.where(slot < live[...], row * 4 + col, 16)
    drawn[pl.ds(0, slots), pl.ds(0, targets)] = position
    square[...] = jnp.full(square.shape, 16, jnp.int32)
    square[pl.ds(0, slots), pl.ds(0, targets)] = position
    turned = square[...].T
    lanes = square.shape[1]
    wide = (targets, lanes)
    behind = lax.broadcasted_iota(jnp.int32, wide, 0) * quads
    ahead = lax.broadcasted_iota(jnp.int32, wide, 1) * quads
    place = lax.broadcasted_iota(jnp.int32, wide, 1)

    def latest(found):
        best = jnp.max(functools.reduce(jnp.maximum, found), axis=0, keepdims=True)
        return jnp.where(best < 0, entries, best)

    for j in range(CHAINS):
        columns = [
            jnp.broadcast_to(turned[:targets, q * CHAINS + j : q * CHAINS + j + 1], wide) for q in range(quads)
        ]
        for q in range(quads):
            k = q * CHAINS + j
            mine = jnp.broadcast_to(square[pl.ds(k, 1), :], wide)
            found = [
                jnp.where((columns[p] == mine) & (behind + p < ahead + q), behind + p, -1)
                for p in range(quads)
            ]
            drawn[pl.ds(slots + k, 1), :] = latest(found)
        found = [jnp.where(columns[p] == place, behind + p, -1) for p in range(quads)]
        drawn[pl.ds(2 * slots + j, 1), :] = latest(found)


def write_out(ocean, adjoint, ocean_hbm, adjoint_hbm, sem):
    size = ocean.shape[2] // PIECES
    copies = [
        pltpu.make_async_copy(
            ocean.at[0, 0, pl.ds(p * size, size)], ocean_hbm.at[0, 0, pl.ds(p * size, size)], sem.at[p]
        )
        for p in range(PIECES)
    ]
    copies.append(pltpu.make_async_copy(adjoint, adjoint_hbm, sem.at[PIECES]))
    for copy in copies:
        copy.start()
    for copy in copies:
        copy.wait()


def body(lat_count, lon_count, increment, cotangent, weights, source_ids, counts):
    targets, slots = weights.shape[2], weights.shape[3]
    rows, cells = increment.shape[2], increment.shape[3]
    groups = targets // GROUP
    entries = targets * slots // CHAINS
    halo = len(HALO)
    any_space = pl.BlockSpec(memory_space=pl.ANY)
    dma = pltpu.SemaphoreType.DMA
    ocean, adjoint = pl.pallas_call(
        functools.partial(kernel, lat_count, lon_count, targets, slots),
        out_shape=(
            pltpu.VMEM(cotangent.shape, jnp.bfloat16),
            pltpu.VMEM(increment.shape, jnp.bfloat16),
        ),
        in_specs=[any_space] * 5,
        out_specs=(pl.BlockSpec(memory_space=pltpu.VMEM),) * 2,
        scratch_shapes=[
            pltpu.VMEM((RING, GROUP, slots, cells, cells), jnp.bfloat16),
            pltpu.VMEM((targets, rows, cells), jnp.bfloat16),
            pltpu.VMEM((17, rows, cells), jnp.bfloat16),
        ]
        + [pltpu.VMEM((entries + 1, rows, cells), jnp.float32)] * CHAINS
        + [
            pltpu.VMEM((halo, rows, cells), jnp.int16),
            pltpu.VMEM((halo, rows, cells), jnp.int16),
            pltpu.VMEM((halo, 8, cells), jnp.float32),
            pltpu.VMEM((halo, 8, cells), jnp.float32),
            pltpu.VMEM((slots, targets), jnp.int32),
            pltpu.VMEM((1, targets), jnp.int32),
            pltpu.VMEM((128, 128), jnp.int32),
            pltpu.VMEM((2 * slots + 8, 128), jnp.int32),
            pltpu.SMEM((2 * slots + 8, 128), jnp.int32),
            dma((RING, GROUP)),
            dma((groups,)),
            dma((2,)),
            dma((halo,)),
            dma((halo,)),
            dma((2, len(PARTS))),
            dma((2, len(PARTS))),
            dma((2,)),
            dma,
        ],
        compiler_params=pltpu.CompilerParams(
            collective_id=0, has_side_effects=True, vmem_limit_bytes=64000000
        ),
    )(increment, cotangent, weights, jnp.swapaxes(source_ids, 2, 3), counts)
    in_vmem = pl.BlockSpec(memory_space=pltpu.VMEM)
    return pl.pallas_call(
        write_out,
        out_shape=(
            jax.ShapeDtypeStruct(ocean.shape, ocean.dtype),
            jax.ShapeDtypeStruct(adjoint.shape, adjoint.dtype),
        ),
        in_specs=[in_vmem, in_vmem],
        out_specs=(any_space, any_space),
        scratch_shapes=[dma((PIECES + 1,))],
        compiler_params=pltpu.CompilerParams(vmem_limit_bytes=4 << 20),
    )(*(pltpu.with_memory_space_constraint(value, pltpu.VMEM) for value in (ocean, adjoint)))


def solution(mesh):
    placed = (
        P("lat", "lon", None, None),
        P("lat", "lon", None, None, None),
        P("lat", "lon", None, None, None, None),
        P("lat", "lon", None, None),
        P("lat", "lon", None),
    )
    return jax.shard_map(
        functools.partial(body, mesh.shape["lat"], mesh.shape["lon"]),
        mesh=mesh,
        in_specs=placed,
        out_specs=(P("lat", "lon", None, None, None), P("lat", "lon", None, None)),
        check_vma=False,
    )
```

time: 35.8 us -> 25.1 us (0.70)
  local copies, waits for them, and re-layouts: 5.72 us -> 0 us
  Pallas kernels: 27.1 us -> 24.1 us
  other arithmetic: 1.97 us -> 0 us
    pallas_call x1, Pallas kernels: 27.1 us -> 22.9 us  [body(): pl.pallas_call(functools.partial(kernel, lat_count, lon_count, targets, s...]
    unnamed x5 -> x0, local copies, waits for them, and re-layouts: 4.06 us -> none
    pallas_call x0 -> x1, Pallas kernels: none -> 1.19 us  [body(): pl.pallas_call(write_out, out_shape=(jax.ShapeDtypeStruct(ocean.shape, oc...]
    lt x5 -> x0, local copies, waits for them, and re-layouts: 1.04 us -> none  [tables(): live = jnp.arange(slots, dtype=jnp.int32)[None, :] < counts[0, 0][:, None]]
    lt x3 -> x0, other arithmetic: 0.76 us -> none  [the longest x2 0.74 us: tables(): live = jnp.arange(slots, dtype=jnp.int32)[None, :] < counts[0, 0][:, None]]
    concatenate x1 -> x0, other arithmetic: 0.61 us -> none  [tables(): jnp.concatenate([position.reshape(-1), before.T.reshape(-1), final.T.resh...]
    reduce_max x2 -> x0, other arithmetic: 0.55 us -> none  [the longest x1 0.4 us: tables(): before = jnp.max(jnp.where(same, order[None, None, :], -1), axis=2)]
where the time goes in v2:
time: 25.1 us; the launch traced here: 24.7 us
  Pallas kernels  24.1 us (96%)
  between operations  0.64 us (3%)
    pallas_call x1, Pallas kernels, body(): pl.pallas_call(functools.partial(kernel, lat_count, lon_count, targets, s...  22.9 us
    pallas_call x1, Pallas kernels, body(): pl.pallas_call(write_out, out_shape=(jax.ShapeDtypeStruct(ocean.shape, oc...  1.19 us

profile of v2, /device:TPU:6, one launch (start us, length us, event | category | flops | bytes accessed | tf_op | source)
XLA Modules:
  0.0 24.7 jit_solution(4568417123829833934)
XLA Ops:
  0.6 22.9 %shard_map.68 = (bf16[1,1,40,144,128]{4,3,2,1,0:T(8,128)(2,1)S(1)}, bf16[2,2,144,128]{3,2,1,0:T(8,128)(2,1)S(1)}) custom-call(bf16[2,2,144,128]{3,2,1,0:T(8,128)(2,1)} %inc_hbm.1, bf16[1,1,40,144,128]{4,3,2,1,0:T(8,128)(2,1)} %cot_hbm.1, bf16[1,1,40,16,128,128]{5,4,3,2,1,0:T(8,128)(2,1)} %w_hbm.1, s32[1,1,16,40]{3,2,1,0:T(8,128)} %bitcast.1, ...), custom_call_target="tpu_custom_call" | custom-call | tf_op jit(solution)/shard_map/pallas_call | solution.py:319
  23.5 1.2 %shard_map.69 = (bf16[1,1,40,144,128]{4,3,2,1,0:T(8,128)(2,1)}, bf16[2,2,144,128]{3,2,1,0:T(8,128)(2,1)}) custom-call(bf16[1,1,40,144,128]{4,3,2,1,0:T(8,128)(2,1)S(1)} %get-tuple-element.4.ocean, bf16[2,2,144,128]{3,2,1,0:T(8,128)(2,1)S(1)} %get-tuple-element.5.adjoint), custom_call_target="tpu_custom_call" | custom-call | tf_op jit(solution)/shard_map/pallas_call | solution.py:358

commit v3 on v2

--- a/solution.py
+++ b/solution.py
@@ -10,7 +10,7 @@
 MESH = pl.DeviceIdType.MESH
 CHAINS = 4
 GROUP = 8
-RING = 2
+RING = 3
 PIECES = 4
 SYNC = 1
 
@@ -351,7 +351,7 @@
             dma,
         ],
         compiler_params=pltpu.CompilerParams(
-            collective_id=0, has_side_effects=True, vmem_limit_bytes=64000000
+            collective_id=0, has_side_effects=True, vmem_limit_bytes=65300000
         ),
     )(increment, cotangent, weights, jnp.swapaxes(source_ids, 2, 3), counts)
     in_vmem = pl.BlockSpec(memory_space=pltpu.VMEM)

time: 25.1 us -> 24 us (0.956); the launches traced: 24.7 us -> 23.9 us
  Pallas kernels: 24.1 us -> 23.3 us
    pallas_call x1, Pallas kernels: 22.9 us -> 22.1 us  [body(): pl.pallas_call(functools.partial(kernel, lat_count, lon_count, targets, s...]
where the time goes in v3:
time: 24 us; the launch traced here: 23.9 us
  Pallas kernels  23.3 us (97%)
  between operations  0.64 us (3%)
    pallas_call x1, Pallas kernels, body(): pl.pallas_call(functools.partial(kernel, lat_count, lon_count, targets, s...  22.1 us
    pallas_call x1, Pallas kernels, body(): pl.pallas_call(write_out, out_shape=(jax.ShapeDtypeStruct(ocean.shape, oc...  1.19 us

profile of v3, /device:TPU:6, one launch (start us, length us, event | category | flops | bytes accessed | tf_op | source)
XLA Modules:
  0.0 23.9 jit_solution(8756610029604006720)
XLA Ops:
  0.6 22.1 %shard_map.68 = (bf16[1,1,40,144,128]{4,3,2,1,0:T(8,128)(2,1)S(1)}, bf16[2,2,144,128]{3,2,1,0:T(8,128)(2,1)S(1)}) custom-call(bf16[2,2,144,128]{3,2,1,0:T(8,128)(2,1)} %inc_hbm.1, bf16[1,1,40,144,128]{4,3,2,1,0:T(8,128)(2,1)} %cot_hbm.1, bf16[1,1,40,16,128,128]{5,4,3,2,1,0:T(8,128)(2,1)} %w_hbm.1, s32[1,1,16,40]{3,2,1,0:T(8,128)} %bitcast.1, ...), custom_call_target="tpu_custom_call" | custom-call | tf_op jit(solution)/shard_map/pallas_call | solution.py:319
  22.7 1.2 %shard_map.69 = (bf16[1,1,40,144,128]{4,3,2,1,0:T(8,128)(2,1)}, bf16[2,2,144,128]{3,2,1,0:T(8,128)(2,1)}) custom-call(bf16[1,1,40,144,128]{4,3,2,1,0:T(8,128)(2,1)S(1)} %get-tuple-element.4.ocean, bf16[2,2,144,128]{3,2,1,0:T(8,128)(2,1)S(1)} %get-tuple-element.5.adjoint), custom_call_target="tpu_custom_call" | custom-call | tf_op jit(solution)/shard_map/pallas_call | solution.py:358

commit v4 on v3

--- a/solution.py
+++ b/solution.py
@@ -15,7 +15,7 @@
 SYNC = 1
 
 PARTS = [
-    [(0, 1), (0, 2)], [(3, 1), (3, 2)], [(0, 0)], [(0, 3)], [(3, 0)], [(3, 3)],
+    [(3, 1), (3, 2)], [(3, 0)], [(3, 3)], [(0, 1), (0, 2)], [(0, 0)], [(0, 3)],
     [(1, 0), (2, 0)], [(1, 3), (2, 3)],
 ]
 HALO = [place for part in PARTS for place in part]
@@ -27,7 +27,7 @@
 def kernel(
     lat_count, lon_count, targets, slots,
     inc_hbm, cot_hbm, w_hbm, ids_hbm, counts_hbm, obuf, abuf,
-    wbuf, cot, ext, d0, d1, d2, d3, sendq, recvq, sends, recvs, ids, live, square, drawn, table,
+    wbuf, cot, ext, d0, d1, d2, d3, sendq, recvq, sends, recvs, mine, ids, live, square, drawn, table,
     w_sem, cot_sem, own_sem, inc_send, inc_recv, adj_send, adj_recv, ids_sem, table_sem,
 ):
     lat = lax.axis_index("lat")
@@ -239,13 +239,16 @@
                 recvq[index[r, c]] = jnp.zeros((rows, cells), recvq.dtype)
                 recvs[index[r, c]] = jnp.zeros(recvs.shape[1:], recvs.dtype)
 
+    for a in range(2):
+        for b in range(2):
+            mine[a, b] = summed((a + 1) * 4 + b + 1)
     for d in range(len(PARTS)):
         dlat, copies = adj_copies(d)
         guarded(-dlat, each(copies, "wait_recv"))
     for a in range(2):
         for b in range(2):
             far_r, far_c = (3 if a == 0 else 0), (3 if b == 0 else 0)
-            value = summed((a + 1) * 4 + b + 1)
+            value = mine[a, b]
             value += decoded(index[far_r, b + 1]) + decoded(index[a + 1, far_c])
             value += decoded(index[far_r, far_c])
             abuf[a, b] = value.astype(abuf.dtype)
@@ -335,6 +338,7 @@
             pltpu.VMEM((halo, rows, cells), jnp.int16),
             pltpu.VMEM((halo, 8, cells), jnp.float32),
             pltpu.VMEM((halo, 8, cells), jnp.float32),
+            pltpu.VMEM((2, 2, rows, cells), jnp.float32),
             pltpu.VMEM((slots, targets), jnp.int32),
             pltpu.VMEM((1, targets), jnp.int32),
             pltpu.VMEM((128, 128), jnp.int32),

time: 24 us -> 24 us (level)
  no operation moved by 1% of the time
where the time goes in v4:
time: 24 us; the launch traced here: 23.8 us
  Pallas kernels  23.2 us (97%)
  between operations  0.64 us (3%)
    pallas_call x1, Pallas kernels, body(): pl.pallas_call(functools.partial(kernel, lat_count, lon_count, targets, s...  22 us
    pallas_call x1, Pallas kernels, body(): pl.pallas_call(write_out, out_shape=(jax.ShapeDtypeStruct(ocean.shape, oc...  1.19 us

profile of v4, /device:TPU:6, one launch (start us, length us, event | category | flops | bytes accessed | tf_op | source)
XLA Modules:
  0.0 23.8 jit_solution(3175773803929285703)
XLA Ops:
  0.6 22.0 %shard_map.68 = (bf16[1,1,40,144,128]{4,3,2,1,0:T(8,128)(2,1)S(1)}, bf16[2,2,144,128]{3,2,1,0:T(8,128)(2,1)S(1)}) custom-call(bf16[2,2,144,128]{3,2,1,0:T(8,128)(2,1)} %inc_hbm.1, bf16[1,1,40,144,128]{4,3,2,1,0:T(8,128)(2,1)} %cot_hbm.1, bf16[1,1,40,16,128,128]{5,4,3,2,1,0:T(8,128)(2,1)} %w_hbm.1, s32[1,1,16,40]{3,2,1,0:T(8,128)} %bitcast.1, ...), custom_call_target="tpu_custom_call" | custom-call | tf_op jit(solution)/shard_map/pallas_call | solution.py:322
  22.6 1.2 %shard_map.69 = (bf16[1,1,40,144,128]{4,3,2,1,0:T(8,128)(2,1)}, bf16[2,2,144,128]{3,2,1,0:T(8,128)(2,1)}) custom-call(bf16[1,1,40,144,128]{4,3,2,1,0:T(8,128)(2,1)S(1)} %get-tuple-element.4.ocean, bf16[2,2,144,128]{3,2,1,0:T(8,128)(2,1)S(1)} %get-tuple-element.5.adjoint), custom_call_target="tpu_custom_call" | custom-call | tf_op jit(solution)/shard_map/pallas_call | solution.py:362
